TPU v7x, 32 devices: a whole 2x2x4 slice. The times are simulated.
32 devices in a mesh: node: 8 (over z, y), local: 4 (over x, core).
Axes of the slice: x: 2, y: 2, z: 4, core: 2. Of those that a mesh axis runs over, the one named last changes fastest.
Arguments:
- tokens: bfloat16 [4096, 7168], P(('node', 'local')), may hold values from -6 to 6
- w_gate: bfloat16 [8, 7168, 1024], P('node', None, 'local'), may hold values from -0.0625 to 0.0625
- w_up: bfloat16 [8, 7168, 1024], P('node', None, 'local'), may hold values from -0.0625 to 0.0625
- w_down: bfloat16 [8, 1024, 7168], P('node', 'local'), may hold values from -0.1875 to 0.1875
- chosen: int32 [8, 48], replicated, may hold values from 0 to 4095, as said below
- counts: int32 [8], replicated, may hold values from 3 to 48, as said below
- gates: float32 [8, 48], replicated, may hold values from 0.2 to 1
Outputs:
- mixed: bfloat16 [4096, 7168], P(('node', 'local'))
Inputs may be any that keep to these rules, and one draw needn't show every extreme that they name: `chosen`: each expert's list holds distinct tokens; in each list at most 3 entries lie in one device's block of 128 consecutive tokens, and for every expert some block holds exactly 3 live entries. `counts`: some expert has exactly 48 live entries.
All inputs are finite; a program needn't handle non-finite values.
Results may differ from a plain program's by a relative error of at most 0.014.
Values may be sent and summed in bfloat16 or wider, within the bound.
A program may use at most 128 MiB of HBM per device.

v0:
```python
import jax
import jax.numpy as jnp
from jax import lax
from jax.sharding import PartitionSpec as P

SLOT = 3


def shards(tokens, w_gate, w_up, w_down, chosen, counts, gates):
    tok_dev = tokens.shape[0]
    width = tokens.shape[1]
    n_node = lax.axis_size("node")
    n_local = lax.axis_size("local")
    devices = n_node * n_local
    cap = chosen.shape[1]
    experts = chosen.shape[0]
    myself = lax.axis_index("node") * n_local + lax.axis_index("local")
    live = jnp.arange(cap, dtype=jnp.int32)[None, :] < counts[:, None]
    owner = chosen // tok_dev
    mine = live & (owner == myself)
    rank = jnp.cumsum(mine.astype(jnp.int32), axis=1) - 1
    select = (
        mine[:, :, None] & (rank[:, :, None] == jnp.arange(SLOT, dtype=jnp.int32)[None, None, :])
    ).astype(jnp.int32)
    position = chosen - owner * tok_dev
    token_slot = jnp.sum(select * position[:, :, None], axis=1)
    present = jnp.sum(select, axis=1)
    outgoing = tokens[token_slot.reshape(-1)].reshape(experts, SLOT, width)
    outgoing = outgoing * present[:, :, None].astype(jnp.bfloat16)
    expert = lax.axis_index("node")
    picked = lax.dynamic_index_in_dim(chosen, expert, 0, keepdims=False)
    count = lax.dynamic_index_in_dim(counts, expert, 0, keepdims=False)
    weight = lax.dynamic_index_in_dim(gates, expert, 0, keepdims=False)
    valid = jnp.arange(cap, dtype=jnp.int32) < count
    holder = picked // tok_dev
    member = (
        (holder[:, None] == jnp.arange(devices, dtype=jnp.int32)[None, :]) & valid[:, None]
    ).astype(jnp.int32)
    order_in = jnp.sum(member * jnp.cumsum(member, axis=0), axis=1) - 1
    column = holder * SLOT + order_in
    table = jnp.sum(
        jnp.where(
            valid[:, None]
            & (column[:, None] == jnp.arange(devices * SLOT, dtype=jnp.int32)[None, :]),
            weight[:, None],
            jnp.float32(0.0),
        ),
        axis=0,
    )
    table = table.reshape(n_node, n_local, SLOT).transpose(1, 0, 2)
    gate_mat = w_gate[0]
    up_mat = w_up[0]
    down_mat = w_down[0]
    ff_dev = gate_mat.shape[1]
    arrived = lax.all_to_all(outgoing, "node", split_axis=0, concat_axis=0, tiled=True)
    piece = lax.all_gather(arrived[None], "local", axis=0, tiled=True)
    flat = piece.reshape(-1, width)
    gate_val = jnp.dot(flat, gate_mat, preferred_element_type=jnp.float32)
    up_val = jnp.dot(flat, up_mat, preferred_element_type=jnp.float32)
    hidden = (jax.nn.silu(gate_val) * up_val).astype(jnp.bfloat16)
    down_hidden = hidden.reshape(piece.shape[0], n_node, SLOT, ff_dev)
    count_rows = down_hidden.shape[0]
    down_val = jnp.dot(
        down_hidden.reshape(-1, ff_dev), down_mat, preferred_element_type=jnp.float32
    )
    down_val = down_val.reshape(count_rows, n_node, SLOT, width)
    partial_value = (down_val * table[:, :, :, None]).astype(jnp.bfloat16)
    summed = lax.psum_scatter(
        partial_value.astype(jnp.float32).astype(jnp.bfloat16),
        "local",
        scatter_dimension=0,
        tiled=True,
    )
    returned = lax.all_to_all(summed, "node", split_axis=1, concat_axis=1, tiled=True)
    answers = returned[0].reshape(experts * SLOT, width)
    placing = (jnp.arange(tok_dev, dtype=jnp.int32)[:, None] == token_slot.reshape(-1)[None, :]) & (
        present.reshape(-1)[None, :] > 0
    )
    mixed = jnp.dot(placing.astype(jnp.bfloat16), answers, preferred_element_type=jnp.float32)
    return mixed.astype(jnp.bfloat16)


def solution(mesh):
    in_specs = (
        P(("node", "local"), None),
        P("node", None, "local"),
        P("node", None, "local"),
        P("node", "local", None),
        P(),
        P(),
        P(),
    )
    out_specs = P(("node", "local"), None)
    return jax.shard_map(shards, mesh=mesh, in_specs=in_specs, out_specs=out_specs, check_vma=False)
```

profile of v0, /device:TPU:0, one launch (start us, length us, event | category | flops | bytes accessed | tf_op | source)
XLA Modules:
  0.0 119.9 jit_solution(16415027315541604071)
XLA Ops:
  6.5 0.9 fusion.25
  7.6 0.7 multiply_subtract_fusion
  8.7 0.8 gather_fusion
  9.8 0.3 broadcast_multiply_fusion
  10.1 20.3 %all_to_all.10 = bf16[8,3,7168]{2,1,0:T(4,128)(2,1)S(1)} all-to-all(bf16[8,3,7168]{2,1,0:T(4,128)(2,1)S(1)} %broadcast_multiply_fusion), channel_id=1, replica_groups=mesh['node'=8,'local'=4] {'node'}, dimensions={0} | all-to-all | bytes 688128 | tf_op jit(solution)/shard_map/all_to_all | solution.py:55
  30.4 0.9 copy.22
  31.3 0.6 dynamic_slice.12
  32.0 0.7 and_select_fusion
  32.6 0.6 iota_compare_fusion.5
  33.5 0.7 dynamic-slice_bitcast_fusion
  34.3 0.7 add_add_fusion
  35.4 13.7 %all-gather.3.cloned.1.call-done = bf16[32,3,7168]{2,0,1:T(8,128)(2,1)} async-done(((bf16[8,3,7168]{2,0,1:T(8,128)(2,1)}), bf16[32,3,7168]{2,0,1:T(8,128)(2,1)}) %all-gather.3.cloned.1.call-update) | async-done | bytes 1376272 | tf_op jit(solution)/shard_map/all_gather | solution.py:56
  49.0 3.7 %copy.23 = bf16[32,3,7168]{2,1,0:T(4,128)(2,1)} copy(bf16[32,3,7168]{2,0,1:T(8,128)(2,1)} %all-gather.3.cloned.1.call-done) | data formatting | bytes 2752512 | tf_op jit(solution)/shard_map/all_gather | solution.py:56
  52.8 3.0 %reshape.117 = bf16[96,7168]{1,0:T(8,128)(2,1)S(1)} reshape(bf16[32,3,7168]{2,1,0:T(4,128)(2,1)} %copy.23) | data formatting | bytes 2752512 | tf_op jit(solution)/shard_map/reshape | solution.py:57
  55.8 2.9 %fusion.4 = f32[96,256]{1,0:T(8,128)S(1)} fusion(bf16[96,7168]{1,0:T(8,128)(2,1)S(1)} %reshape.117, bf16[1,7168,256]{2,1,0:T(8,128)(2,1)} %param.8), kind=kOutput, calls=%fused_computation.7 | convolution fusion | flops 352321536 | bytes 5144576 | tf_op jit(solution)/shard_map/dot_general | solution.py:58
  58.7 0.2 copy-done.1
  58.9 0.7 fusion.9
  59.7 3.8 %fusion = bf16[4,8,3,7168]{3,1,2,0:T(8,128)(2,1)} fusion(bf16[1,256,7168]{2,1,0:T(8,128)(2,1)} %param.10, f32[4,8,3]{1,2,0:T(4,128)S(1)} %copy.25, bf16[4,8,3,256]{3,2,1,0:T(4,128)(2,1)S(1)} %dot_general.16), kind=kOutput, calls=%fused_computation.3 | convolution fusion | flops 353697792 | bytes 5095808 | tf_op jit(solution)/shard_map/dot_general | solution.py:63
  63.6 26.9 %reduce-scatter.2.cloned.1.call-done = bf16[1,8,3,7168]{3,1,2,0:T(8,128)(2,1)} async-done(((bf16[4,8,3,7168]{3,1,2,0:T(8,128)(2,1)}), bf16[1,8,3,7168]{3,1,2,0:T(8,128)(2,1)}) %reduce-scatter.2.cloned.1.call-update) | async-done | bytes 344080 | tf_op jit(solution)/shard_map/reduce_scatter | solution.py:68
  90.4 2.0 %copy.26 = bf16[1,8,3,7168]{3,2,0,1:T(4,128)(2,1)} copy(bf16[1,8,3,7168]{3,1,2,0:T(8,128)(2,1)} %reduce-scatter.2.cloned.1.call-done) | data formatting | bytes 688128 | tf_op jit(solution)/shard_map/reduce_scatter | solution.py:68
  92.5 5.5 %all-to-all-start.1 = ((bf16[1,8,3,7168]{3,2,0,1:T(4,128)(2,1)}), bf16[1,8,3,7168]{3,2,0,1:T(4,128)(2,1)S(1)}, u32[]{:S(2)}, u32[]{:S(2)}) async-start(bf16[1,8,3,7168]{3,2,0,1:T(4,128)(2,1)} %copy.26), calls=%async_computation.2 | async-start | bytes 917504 | tf_op jit(solution)/shard_map/all_to_all | solution.py:74
  98.3 12.7 %all-to-all-done.1 = bf16[1,8,3,7168]{3,2,0,1:T(4,128)(2,1)S(1)} async-done(((bf16[1,8,3,7168]{3,2,0,1:T(4,128)(2,1)}), bf16[1,8,3,7168]{3,2,0,1:T(4,128)(2,1)S(1)}, u32[]{:S(2)}, u32[]{:S(2)}) %all-to-all-start.1) | async-done | bytes 344096 | tf_op jit(solution)/shard_map/all_to_all | solution.py:74
  110.9 0.3 reshape_squeeze.3
  111.2 1.9 %convolution_convert_fusion = bf16[128,7168]{1,0:T(8,128)(2,1)} fusion(bf16[24,7168]{1,0:T(8,128)(2,1)S(1)} %reshape_squeeze.3, s32[24]{0:T(128)S(1)} %eq.66, pred[24]{0:T(512)(128)(4,1)S(1)} %gt.12), kind=kOutput, calls=%fused_computation.1 | convolution fusion | flops 44963840 | bytes 2179192 | tf_op jit(solution)/shard_map/dot_general | solution.py:79
  (29 shorter events, 1.9 us)
Async XLA Ops:
  6.5 2.2 %copy-start = (bf16[128,7168]{1,0:T(8,128)(2,1)S(1)}, bf16[128,7168]{1,0:T(8,128)(2,1)}, u32[]{:S(2)}) copy-start(bf16[128,7168]{1,0:T(8,128)(2,1)} %param.7) | copy-start | bytes 5505028
  6.5 42.5 %all-gather.3.cloned.1.call-start = ((), (), s32[]{:S(2)}) async-start(), calls=%async_computation.4 | async-start | bytes 1720320 | tf_op jit(solution)/shard_map/all_gather | solution.py:56
  8.7 22.6 %copy-start.2 = (s32[8]{0:T(128)S(1)}, s32[8]{0:T(128)}, u32[]{:S(2)}) copy-start(s32[8]{0:T(128)} %param.12) | copy-start | bytes 100
  31.3 59.2 %reduce-scatter.2.cloned.1.call-start = ((), (), s32[]{:S(2)}) async-start(), calls=%async_computation.3 | async-start | bytes 1720320 | tf_op jit(solution)/shard_map/reduce_scatter | solution.py:68
  55.8 3.1 %copy-start.1 = (bf16[1,7168,256]{2,1,0:T(8,128)(2,1)S(1)}, bf16[1,7168,256]{2,1,0:T(8,128)(2,1)}, u32[]{:S(2)}) copy-start(bf16[1,7168,256]{2,1,0:T(8,128)(2,1)} %param.9) | copy-start | bytes 11010052
  92.5 18.4 %all-to-all-start.1 = ((bf16[1,8,3,7168]{3,2,0,1:T(4,128)(2,1)}), bf16[1,8,3,7168]{3,2,0,1:T(4,128)(2,1)S(1)}, u32[]{:S(2)}, u32[]{:S(2)}) async-start(bf16[1,8,3,7168]{3,2,0,1:T(4,128)(2,1)} %copy.26), calls=%async_computation.2 | async-start | bytes 917504 | tf_op jit(solution)/shard_map/all_to_all | solution.py:74
Sparse Core Ops, SparseCore 0:
  31.4 17.5 all-gather.2
  63.7 26.7 reduce-scatter.1
where the time goes:
time: 120 us
  waiting for transfers between devices  53.3 us (44%)
  blocking collectives  20.3 us (17%)
  between operations  13.5 us (11%)
  local copies, waits for them, and re-layouts  13.2 us (11%)
  matrix products  9.34 us (8%)
  starting transfers between devices  5.55 us (5%)
  other arithmetic  4.75 us (4%)
    reduce_scatter x1, waiting for transfers between devices, shards(): lax.psum_scatter(partial_value.astype(jnp.float32).astype(jnp.bfloat16),...  26.9 us
    all_to_all x1, blocking collectives, shards(): lax.all_to_all(outgoing, 'node', split_axis=0, concat_axis=0, tiled=True)  20.3 us
    all_gather x1, waiting for transfers between devices, shards(): piece = lax.all_gather(arrived[None], 'local', axis=0, tiled=True)  13.7 us
    all_to_all x1, waiting for transfers between devices, shards(): lax.all_to_all(summed, 'node', split_axis=1, concat_axis=1, tiled=True)  12.7 us
    all_to_all x1, starting transfers between devices, shards(): lax.all_to_all(summed, 'node', split_axis=1, concat_axis=1, tiled=True)  5.51 us
    dot_general x1, matrix products, shards(): jnp.dot(down_hidden.reshape(-1, ff_dev), down_mat, preferred_element_type...  3.84 us
    all_gather x1, local copies, waits for them, and re-layouts, shards(): piece = lax.all_gather(arrived[None], 'local', axis=0, tiled=True)  3.75 us
    reshape x1, local copies, waits for them, and re-layouts, shards(): flat = piece.reshape(-1, width)  2.97 us
  transfers between devices with their start and end apart: 3, of which 3 were waited for; matrix products, arithmetic and copies ran while one was open for 4% of the time, Pallas kernels for 0%

commit v1 on v0

v1 whole, which is shorter than its diff:
```python
import functools

import jax
import jax.numpy as jnp
from jax import lax
from jax.experimental import pallas as pl
from jax.experimental.pallas import tpu as pltpu
from jax.sharding import PartitionSpec as P

SLOT = 3
SUB, LANE = 8, 128
COLS = SUB * LANE
MESH = pl.DeviceIdType.MESH
DISPATCH_GROUPS = 2
COMBINE_GROUPS = 4


def split(count, groups):
    groups = min(groups, count)
    sizes = [count // groups + (1 if g < count % groups else 0) for g in range(groups)]
    starts = [sum(sizes[:g]) for g in range(groups)]
    return list(zip(starts, sizes))


def kernel(dims, counts_ref, chosen_ref, gates_ref, tokens_ref, wg_hbm, wu_hbm, wd_hbm, out_ref,
           wg, wu, wd, tx, rx, py, r1b, s2, r2b, a3, ax, stage,
           wsem, lsem, bsem, d1s, d1r, d2s, d2r, d3s, d3r, d4s, d4r, r1s, r1r, r2s, r2r, r3s, r3r):
    n_node, n_local, chunks, tok_dev, ff = dims
    nx = n_local // 2
    experts, cap = chosen_ref.shape
    per = n_node * SLOT
    rows = n_local * per
    f32, bf16 = jnp.float32, jnp.bfloat16
    me_n, me_l = lax.axis_index("node"), lax.axis_index("local")
    me_x, me_c = me_l // 2, me_l % 2
    partner = me_x * 2 + (1 - me_c)
    dgroups, cgroups = split(chunks, DISPATCH_GROUPS), split(chunks, COMBINE_GROUPS)

    def node_at(k):
        return lax.rem(me_n + k + n_node, n_node)

    def x_at(k):
        return lax.rem(me_x + k + nx, nx)

    def remote(src, dst, ssem, rsem, node, local):
        return pltpu.make_async_remote_copy(
            src_ref=src, dst_ref=dst, send_sem=ssem, recv_sem=rsem,
            device_id=(node, local), device_id_type=MESH)

    sent = []

    def send(*args):
        copy = remote(*args)
        copy.start()
        sent.append(copy)

    barrier = pltpu.get_barrier_semaphore()
    for k in range(1, n_node):
        pl.semaphore_signal(barrier, inc=1, device_id=(node_at(k), me_l), device_id_type=MESH)
    pl.semaphore_signal(barrier, inc=1, device_id=(me_n, partner), device_id_type=MESH)
    for k in range(1, nx):
        pl.semaphore_signal(barrier, inc=1, device_id=(me_n, x_at(k) * 2 + me_c), device_id_type=MESH)

    loads = [pltpu.make_async_copy(src.at[0], dst, wsem.at[i])
             for i, (src, dst) in enumerate(((wg_hbm, wg), (wu_hbm, wu), (wd_hbm, wd)))]
    for copy in loads:
        copy.start()

    base = (me_n * n_local + me_l) * tok_dev
    row = lax.broadcasted_iota(jnp.int32, (experts, cap), 0)
    count = jnp.zeros((experts, cap), jnp.int32)
    for e in range(experts):
        count = jnp.where(row == e, counts_ref[e], count)
    pos = chosen_ref[...] - base
    mine = (lax.broadcasted_iota(jnp.int32, (experts, cap), 1) < count) & (pos >= 0) & (pos < tok_dev)
    before = (lax.broadcasted_iota(jnp.int32, (cap, cap), 0)
              < lax.broadcasted_iota(jnp.int32, (cap, cap), 1))
    rank = jnp.dot(jnp.where(mine, 1.0, 0.0).astype(bf16), jnp.where(before, 1.0, 0.0).astype(bf16),
                   preferred_element_type=f32)
    pos1 = (pos + 1).astype(f32)
    lane1 = (lax.broadcasted_iota(jnp.int32, (experts, tok_dev), 1) + 1).astype(f32)
    picks, weights = [], []
    for s in range(SLOT):
        sel = mine & (rank == float(s))
        where = jnp.sum(jnp.where(sel, pos1, 0.0), axis=1, keepdims=True)
        gate = jnp.sum(jnp.where(sel, gates_ref[...], 0.0), axis=1, keepdims=True)
        hit = lane1 == where
        picks.append(jnp.where(hit, 1.0, 0.0))
        weights.append(jnp.where(hit, gate, 0.0))
    pick = jnp.concatenate(picks, axis=0)
    weight = jnp.concatenate(weights, axis=0)
    col = lax.broadcasted_iota(jnp.int32, (per, per), 1)
    slot = jnp.zeros((per, per), jnp.int32)
    for s in range(1, SLOT):
        slot = slot + jnp.where(col >= s * experts, 1, 0)
    order = lax.broadcasted_iota(jnp.int32, (per, per), 0) == (col - slot * experts) * SLOT + slot
    order = jnp.where(order, 1.0, 0.0).astype(bf16)
    high = weight.astype(bf16)
    low = (weight - high.astype(f32)).astype(bf16)

    def ordered(x):
        return jnp.dot(order, x, preferred_element_type=f32)

    select = ordered(pick.astype(bf16)).astype(bf16)
    high_t = jnp.transpose(ordered(high)).astype(bf16)
    low_t = jnp.transpose(ordered(low)).astype(bf16)

    def to_tiles(value, m):
        for q in range(SUB):
            stage[pl.ds(q, m, stride=SUB), :] = value[:, q * LANE:(q + 1) * LANE]
        return stage[pl.ds(0, m * SUB), :].astype(bf16).reshape(m, SUB, LANE)

    def from_tiles(value, m):
        stage[pl.ds(0, m * SUB), :] = value.reshape(m * SUB, LANE).astype(f32)
        return jnp.concatenate(
            [stage[pl.ds(q, m, stride=SUB), :].astype(bf16) for q in range(SUB)], axis=1)

    mine_rows = pl.ds(me_n * SLOT, SLOT)
    far_first = list(range(1, n_node))
    far_first.sort(key=lambda k: -min(k, n_node - k))
    own = []
    for g, (j0, jn) in enumerate(dgroups):
        js = pl.ds(j0, jn)
        for j in range(j0, j0 + jn):
            picked = jnp.dot(select, tokens_ref[:, j * COLS:(j + 1) * COLS], preferred_element_type=f32)
            tx[j] = to_tiles(picked, per)
        if g == 0:
            pl.semaphore_wait(barrier, n_node - 1 + 1 + nx - 1)
        for k in far_first:
            dst = node_at(k)
            send(tx.at[js, pl.ds(dst * SLOT, SLOT)], rx.at[js, me_l, mine_rows],
                 d1s.at[g, k], d1r.at[g, k], dst, me_l)
        copy = pltpu.make_async_copy(tx.at[js, mine_rows], rx.at[js, me_l, mine_rows], lsem.at[g])
        copy.start()
        own.append(copy)

    near_first = [0] + far_first[::-1]

    def block(js, local, node):
        return rx.at[js, local, pl.ds(node * SLOT, SLOT)]

    def pass_on(g):
        j0, jn = dgroups[g]
        js = pl.ds(j0, jn)
        for k in near_first:
            src = node_at(-k)
            here = block(js, me_l, src)
            if k == 0:
                out = tx.at[js, mine_rows]
            else:
                remote(here, here, d1s.at[g, k], d1r.at[g, k], me_n, partner).wait_recv()
                out = here
            for d in range(1, nx):
                send(out, here, d2s.at[g, k, d], d2r.at[g, k, d], me_n, x_at(d) * 2 + me_c)
            send(out, here, d3s.at[g, k], d3r.at[g, k], me_n, partner)

    def pass_across(g):
        j0, jn = dgroups[g]
        js = pl.ds(j0, jn)
        for k in near_first:
            src = node_at(-k)
            for d in range(1, nx):
                here = block(js, x_at(-d) * 2 + me_c, src)
                remote(here, here, d2s.at[g, k, d], d2r.at[g, k, d], me_n, partner).wait_recv()
                send(here, here, d4s.at[g, k, d], d4r.at[g, k, d], me_n, partner)

    def wait_rest(g):
        j0, jn = dgroups[g]
        js = pl.ds(j0, jn)
        own[g].wait()
        for k in near_first:
            src = node_at(-k)
            here = block(js, partner, src)
            remote(here, here, d3s.at[g, k], d3r.at[g, k], me_n, partner).wait_recv()
            for d in range(1, nx):
                here = block(js, x_at(-d) * 2 + (1 - me_c), src)
                remote(here, here, d4s.at[g, k, d], d4r.at[g, k, d], me_n, partner).wait_recv()

    acc = (jnp.zeros((rows, ff), f32), jnp.zeros((rows, ff), f32))

    def first_matmuls(g, acc):
        j0, jn = dgroups[g]

        def step(j, acc):
            x = from_tiles(rx[j].reshape(rows, SUB, LANE), rows)
            ks = pl.ds(pl.multiple_of(j * COLS, COLS), COLS)
            return (acc[0] + jnp.dot(x, wg[ks, :], preferred_element_type=f32),
                    acc[1] + jnp.dot(x, wu[ks, :], preferred_element_type=f32))
        return lax.fori_loop(j0, j0 + jn, step, acc)

    for g in range(len(dgroups)):
        pass_on(g)
        if g > 0:
            pass_across(g - 1)
    pass_across_last = len(dgroups) - 1
    for g in range(len(dgroups)):
        if g == pass_across_last:
            pass_across(g)
        wait_rest(g)
        if g == 0:
            loads[0].wait()
            loads[1].wait()
        acc = first_matmuls(g, acc)
    hidden = (acc[0] / (1.0 + jnp.exp(-acc[0])) * acc[1]).astype(bf16)
    loads[2].wait()

    octs = per // SUB
    for g, (j0, jn) in enumerate(cgroups):
        js = pl.ds(j0, jn)
        for j in range(j0, j0 + jn):
            y = jnp.dot(hidden, wd[:, j * COLS:(j + 1) * COLS], preferred_element_type=f32)
            py[j] = y.reshape(n_local, octs, SUB, COLS).astype(bf16)
        for xx in range(nx):
            send(py.at[js, xx * 2 + (1 - me_c)], r1b.at[js, xx], r1s.at[g, xx], r1r.at[g, xx], me_n, partner)
    for g, (j0, jn) in enumerate(cgroups):
        js = pl.ds(j0, jn)
        for xx in range(nx):
            there = r1b.at[js, xx]
            remote(there, there, r1s.at[g, xx], r1r.at[g, xx], me_n, partner).wait_recv()
        for d in range(1, nx):
            xd = x_at(d)
            for j in range(j0, j0 + jn):
                s2[j, d - 1] = (py[j, xd * 2 + me_c].astype(f32) + r1b[j, xd].astype(f32)).astype(bf16)
            send(s2.at[js, d - 1], r2b.at[js, d - 1], r2s.at[g, d], r2r.at[g, d], me_n, xd * 2 + me_c)
    back = []
    for g, (j0, jn) in enumerate(cgroups):
        js = pl.ds(j0, jn)
        for d in range(1, nx):
            there = r2b.at[js, d - 1]
            remote(there, there, r2s.at[g, d], r2r.at[g, d], me_n, partner).wait_recv()
        for j in range(j0, j0 + jn):
            total = py[j, me_l].astype(f32) + r1b[j, me_x].astype(f32)
            for d in range(1, nx):
                total = total + r2b[j, d - 1].astype(f32)
            a3[j] = to_tiles(total.reshape(per, COLS), per)
        for k in far_first:
            dst = node_at(k)
            send(a3.at[js, pl.ds(dst * SLOT, SLOT)], ax.at[js, mine_rows],
                 r3s.at[g, k], r3r.at[g, k], dst, me_l)
        copy = pltpu.make_async_copy(a3.at[js, mine_rows], ax.at[js, mine_rows], bsem.at[g])
        copy.start()
        back.append(copy)
    for g, (j0, jn) in enumerate(cgroups):
        js = pl.ds(j0, jn)
        back[g].wait()
        for k in near_first[1:]:
            there = ax.at[js, pl.ds(node_at(-k) * SLOT, SLOT)]
            remote(there, there, r3s.at[g, k], r3r.at[g, k], me_n, partner).wait_recv()
        for j in range(j0, j0 + jn):
            answers = from_tiles(ax[j], per)
            mixed = (jnp.dot(high_t, answers, preferred_element_type=f32)
                     + jnp.dot(low_t, answers, preferred_element_type=f32))
            out_ref[:, j * COLS:(j + 1) * COLS] = mixed.astype(bf16)
    for copy in sent:
        copy.wait_send()


def shards(n_node, n_local, tokens, w_gate, w_up, w_down, chosen, counts, gates):
    tok_dev, width = tokens.shape
    ff = w_gate.shape[2]
    chunks = width // COLS
    nx = n_local // 2
    per = n_node * SLOT
    octs = per // SUB
    rows = n_local * per
    dg, cg = len(split(chunks, DISPATCH_GROUPS)), len(split(chunks, COMBINE_GROUPS))
    bf16 = jnp.bfloat16
    vmem = pl.BlockSpec(memory_space=pltpu.VMEM)
    dma = pltpu.SemaphoreType.DMA
    xs = max(nx - 1, 1)
    return pl.pallas_call(
        functools.partial(kernel, (n_node, n_local, chunks, tok_dev, ff)),
        out_shape=jax.ShapeDtypeStruct((tok_dev, width), bf16),
        in_specs=[pl.BlockSpec(memory_space=pltpu.SMEM), vmem, vmem, vmem]
        + [pl.BlockSpec(memory_space=pl.ANY)] * 3,
        out_specs=vmem,
        scratch_shapes=[
            pltpu.VMEM((width, ff), bf16),
            pltpu.VMEM((width, ff), bf16),
            pltpu.VMEM((ff, width), bf16),
            pltpu.VMEM((chunks, per, SUB, LANE), bf16),
            pltpu.VMEM((chunks, n_local, per, SUB, LANE), bf16),
            pltpu.VMEM((chunks, n_local, octs, SUB, COLS), bf16),
            pltpu.VMEM((chunks, nx, octs, SUB, COLS), bf16),
            pltpu.VMEM((chunks, xs, octs, SUB, COLS), bf16),
            pltpu.VMEM((chunks, xs, octs, SUB, COLS), bf16),
            pltpu.VMEM((chunks, per, SUB, LANE), bf16),
            pltpu.VMEM((chunks, per, SUB, LANE), bf16),
            pltpu.VMEM((rows * SUB, LANE), jnp.float32),
            dma((3,)), dma((dg,)), dma((cg,)),
            dma((dg, n_node)), dma((dg, n_node)),
            dma((dg, n_node, nx)), dma((dg, n_node, nx)),
            dma((dg, n_node)), dma((dg, n_node)),
            dma((dg, n_node, nx)), dma((dg, n_node, nx)),
            dma((cg, nx)), dma((cg, nx)),
            dma((cg, nx)), dma((cg, nx)),
            dma((cg, n_node)), dma((cg, n_node)),
        ],
        compiler_params=pltpu.CompilerParams(
            collective_id=0, has_side_effects=True, vmem_limit_bytes=66000000),
    )(counts, chosen, gates, tokens, w_gate, w_up, w_down)


def solution(mesh):
    in_specs = (
        P(("node", "local"), None),
        P("node", None, "local"),
        P("node", None, "local"),
        P("node", "local", None),
        P(),
        P(),
        P(),
    )
    out_specs = P(("node", "local"), None)
    body = functools.partial(shards, mesh.shape["node"], mesh.shape["local"])
    return jax.shard_map(body, mesh=mesh, in_specs=in_specs, out_specs=out_specs, check_vma=False)
```

time: 120 us -> 47.3 us (0.39)
  waiting for transfers between devices: 53.3 us -> 0 us
  Pallas kernels: 0 us -> 44.2 us
  blocking collectives: 20.3 us -> 0 us
  between operations: 13.5 us -> 0.01 us
  local copies, waits for them, and re-layouts: 13.2 us -> 2.85 us
  matrix products: 9.34 us -> 0 us
  starting transfers between devices: 5.55 us -> 0 us
  other arithmetic: 4.75 us -> 0 us
    pallas_call x0 -> x1, Pallas kernels: none -> 44.2 us  [shards(): pl.pallas_call(functools.partial(kernel, (n_node, n_local, chunks, tok_de...]
    reduce_scatter x1 -> x0, waiting for transfers between devices: 26.9 us -> none  [shards(): lax.psum_scatter(partial_value.astype(jnp.float32).astype(jnp.bfloat16),...]
    all_to_all x1 -> x0, blocking collectives: 20.3 us -> none  [shards(): lax.all_to_all(outgoing, 'node', split_axis=0, concat_axis=0, tiled=True)]
    all_gather x1 -> x0, waiting for transfers between devices: 13.7 us -> none  [shards(): piece = lax.all_gather(arrived[None], 'local', axis=0, tiled=True)]
    all_to_all x1 -> x0, waiting for transfers between devices: 12.7 us -> none  [shards(): lax.all_to_all(summed, 'node', split_axis=1, concat_axis=1, tiled=True)]
    dot_general x4 -> x0, matrix products: 9.34 us -> none  [the longest x1 3.84 us: shards(): jnp.dot(down_hidden.reshape(-1, ff_dev), down_mat, preferred_element_type...]
    all_to_all x1 -> x0, starting transfers between devices: 5.51 us -> none  [shards(): lax.all_to_all(summed, 'node', split_axis=1, concat_axis=1, tiled=True)]
    all_gather x1 -> x0, local copies, waits for them, and re-layouts: 3.75 us -> none  [shards(): piece = lax.all_gather(arrived[None], 'local', axis=0, tiled=True)]
  transfers between devices with their start and end apart: 3 -> 0, of which waited for: 3 -> 0; matrix products, arithmetic and copies ran while one was open for 4% -> 0% of each run, Pallas kernels for 0% -> 0%
where the time goes in v1:
time: 47.3 us; the launch traced here: 47.1 us
  Pallas kernels  44.2 us (93%)
  local copies, waits for them, and re-layouts  2.85 us (6%)
    pallas_call x1, Pallas kernels, shards(): pl.pallas_call(functools.partial(kernel, (n_node, n_local, chunks, tok_de...  44.2 us
    unnamed x1, local copies, waits for them, and re-layouts  2.85 us

profile of v1, /device:TPU:0, one launch (start us, length us, event | category | flops | bytes accessed | tf_op | source)
XLA Modules:
  0.0 47.1 jit_solution(14422187449994032275)
XLA Ops:
  0.0 44.2 %shard_map.73 = bf16[128,7168]{1,0:T(8,128)(2,1)} custom-call(s32[8]{0:T(128)} %counts_ref.1, s32[8,48]{1,0:T(8,128)} %chosen_ref.1, f32[8,48]{1,0:T(8,128)} %gates_ref.1, bf16[128,7168]{1,0:T(8,128)(2,1)} %tokens_ref.1, bf16[1,7168,256]{2,1,0:T(8,128)(2,1)} %wg_hbm.1, bf16[1,7168,256]{2,1,0:T(8,128)(2,1)} %wu_hbm.1, bf16[1,256,7168]{2,1,0:T(8,128)(2,1)} %wd_hbm.1), custom_call_target="tpu_custom_call" | custom-call | tf_op jit(solution)/shard_map/pallas_call | solution.py:271
  44.2 2.8 %copy.9 = bf16[128,7168]{1,0:T(8,128)(2,1)} copy(bf16[128,7168]{1,0:T(8,128)(2,1)} %shard_map.73) | data formatting | bytes 3670016

commit v2 on v1

--- a/solution.py
+++ b/solution.py
@@ -11,7 +11,7 @@
 SUB, LANE = 8, 128
 COLS = SUB * LANE
 MESH = pl.DeviceIdType.MESH
-DISPATCH_GROUPS = 2
+DISPATCH_GROUPS = 1
 COMBINE_GROUPS = 4
 
 
@@ -22,21 +22,26 @@
     return list(zip(starts, sizes))
 
 
-def kernel(dims, counts_ref, chosen_ref, gates_ref, tokens_ref, wg_hbm, wu_hbm, wd_hbm, out_ref,
-           wg, wu, wd, tx, rx, py, r1b, s2, r2b, a3, ax, stage,
+def kernel(dims, counts_hbm, chosen_hbm, gates_hbm, tokens_hbm, wg_hbm, wu_hbm, wd_hbm, out_ref, place_ref,
+           counts_ref, chosen_ref, gates_ref, tokens_ref, wg, wu, wd, tx, rx, py, r1b, s2, r2b, a3, ax, stage,
            wsem, lsem, bsem, d1s, d1r, d2s, d2r, d3s, d3r, d4s, d4r, r1s, r1r, r2s, r2r, r3s, r3r):
     n_node, n_local, chunks, tok_dev, ff = dims
     nx = n_local // 2
     experts, cap = chosen_ref.shape
     per = n_node * SLOT
     rows = n_local * per
+    padded = out_ref.shape[0] // 2
     f32, bf16 = jnp.float32, jnp.bfloat16
     me_n, me_l = lax.axis_index("node"), lax.axis_index("local")
     me_x, me_c = me_l // 2, me_l % 2
     partner = me_x * 2 + (1 - me_c)
     dgroups, cgroups = split(chunks, DISPATCH_GROUPS), split(chunks, COMBINE_GROUPS)
 
+    paired = n_node & (n_node - 1) == 0
+
     def node_at(k):
+        if paired:
+            return jnp.bitwise_xor(me_n, abs(k))
         return lax.rem(me_n + k + n_node, n_node)
 
     def x_at(k):
@@ -61,10 +66,13 @@
     for k in range(1, nx):
         pl.semaphore_signal(barrier, inc=1, device_id=(me_n, x_at(k) * 2 + me_c), device_id_type=MESH)
 
-    loads = [pltpu.make_async_copy(src.at[0], dst, wsem.at[i])
-             for i, (src, dst) in enumerate(((wg_hbm, wg), (wu_hbm, wu), (wd_hbm, wd)))]
-    for copy in loads:
+    loads = [pltpu.make_async_copy(src, dst, wsem.at[i]) for i, (src, dst) in enumerate((
+        (wg_hbm.at[0], wg), (wu_hbm.at[0], wu), (wd_hbm.at[0], wd), (tokens_hbm, tokens_ref),
+        (counts_hbm, counts_ref), (chosen_hbm, chosen_ref), (gates_hbm, gates_ref)))]
+    for copy in loads[4:] + [loads[3]] + loads[:3]:
         copy.start()
+    for copy in loads[4:]:
+        copy.wait()
 
     base = (me_n * n_local + me_l) * tok_dev
     row = lax.broadcasted_iota(jnp.int32, (experts, cap), 0)
@@ -102,8 +110,11 @@
         return jnp.dot(order, x, preferred_element_type=f32)
 
     select = ordered(pick.astype(bf16)).astype(bf16)
-    high_t = jnp.transpose(ordered(high)).astype(bf16)
-    low_t = jnp.transpose(ordered(low)).astype(bf16)
+    fill = jnp.zeros((padded - per, tok_dev), f32)
+    parts = [ordered(high), fill, ordered(low), fill] if padded > per else [ordered(high), ordered(low)]
+    place_ref[...] = jnp.transpose(jnp.concatenate(parts, axis=0)).astype(bf16)
+    if padded > per:
+        out_ref[...] = jnp.zeros_like(out_ref)
 
     def to_tiles(value, m):
         for q in range(SUB):
@@ -116,9 +127,10 @@
             [stage[pl.ds(q, m, stride=SUB), :].astype(bf16) for q in range(SUB)], axis=1)
 
     mine_rows = pl.ds(me_n * SLOT, SLOT)
-    far_first = list(range(1, n_node))
-    far_first.sort(key=lambda k: -min(k, n_node - k))
+    near_first = list(range(n_node))
+    far_first = near_first[:0:-1]
     own = []
+    loads[3].wait()
     for g, (j0, jn) in enumerate(dgroups):
         js = pl.ds(j0, jn)
         for j in range(j0, j0 + jn):
@@ -126,7 +138,7 @@
             tx[j] = to_tiles(picked, per)
         if g == 0:
             pl.semaphore_wait(barrier, n_node - 1 + 1 + nx - 1)
-        for k in far_first:
+        for k in near_first[1:]:
             dst = node_at(k)
             send(tx.at[js, pl.ds(dst * SLOT, SLOT)], rx.at[js, me_l, mine_rows],
                  d1s.at[g, k], d1r.at[g, k], dst, me_l)
@@ -134,7 +146,6 @@
         copy.start()
         own.append(copy)
 
-    near_first = [0] + far_first[::-1]
 
     def block(js, local, node):
         return rx.at[js, local, pl.ds(node * SLOT, SLOT)]
@@ -248,11 +259,17 @@
             remote(there, there, r3s.at[g, k], r3r.at[g, k], me_n, partner).wait_recv()
         for j in range(j0, j0 + jn):
             answers = from_tiles(ax[j], per)
-            mixed = (jnp.dot(high_t, answers, preferred_element_type=f32)
-                     + jnp.dot(low_t, answers, preferred_element_type=f32))
-            out_ref[:, j * COLS:(j + 1) * COLS] = mixed.astype(bf16)
+            out_ref[0:per, j * COLS:(j + 1) * COLS] = answers
+            out_ref[padded:padded + per, j * COLS:(j + 1) * COLS] = answers
     for copy in sent:
         copy.wait_send()
+
+
+def mix(place_ref, answers_ref, out_ref):
+    answers = answers_ref[...]
+    mixed = (jnp.dot(place_ref[0], answers, preferred_element_type=jnp.float32)
+             + jnp.dot(place_ref[1], answers, preferred_element_type=jnp.float32))
+    out_ref[...] = mixed.astype(out_ref.dtype)
 
 
 def shards(n_node, n_local, tokens, w_gate, w_up, w_down, chosen, counts, gates):
@@ -262,19 +279,23 @@
     nx = n_local // 2
     per = n_node * SLOT
     octs = per // SUB
+    padded = -(-per // 16) * 16
     rows = n_local * per
     dg, cg = len(split(chunks, DISPATCH_GROUPS)), len(split(chunks, COMBINE_GROUPS))
     bf16 = jnp.bfloat16
     vmem = pl.BlockSpec(memory_space=pltpu.VMEM)
     dma = pltpu.SemaphoreType.DMA
     xs = max(nx - 1, 1)
-    return pl.pallas_call(
+    answers, place = pl.pallas_call(
         functools.partial(kernel, (n_node, n_local, chunks, tok_dev, ff)),
-        out_shape=jax.ShapeDtypeStruct((tok_dev, width), bf16),
-        in_specs=[pl.BlockSpec(memory_space=pltpu.SMEM), vmem, vmem, vmem]
-        + [pl.BlockSpec(memory_space=pl.ANY)] * 3,
-        out_specs=vmem,
+        out_shape=(jax.ShapeDtypeStruct((2 * padded, width), bf16), jax.ShapeDtypeStruct((tok_dev, 2 * padded), bf16)),
+        in_specs=[pl.BlockSpec(memory_space=pl.ANY)] * 7,
+        out_specs=(vmem, vmem),
         scratch_shapes=[
+            pltpu.SMEM(counts.shape, counts.dtype),
+            pltpu.VMEM(chosen.shape, chosen.dtype),
+            pltpu.VMEM(gates.shape, gates.dtype),
+            pltpu.VMEM((tok_dev, width), bf16),
             pltpu.VMEM((width, ff), bf16),
             pltpu.VMEM((width, ff), bf16),
             pltpu.VMEM((ff, width), bf16),
@@ -287,7 +308,7 @@
             pltpu.VMEM((chunks, per, SUB, LANE), bf16),
             pltpu.VMEM((chunks, per, SUB, LANE), bf16),
             pltpu.VMEM((rows * SUB, LANE), jnp.float32),
-            dma((3,)), dma((dg,)), dma((cg,)),
+            dma((7,)), dma((dg,)), dma((cg,)),
             dma((dg, n_node)), dma((dg, n_node)),
             dma((dg, n_node, nx)), dma((dg, n_node, nx)),
             dma((dg, n_node)), dma((dg, n_node)),
@@ -299,6 +320,7 @@
         compiler_params=pltpu.CompilerParams(
             collective_id=0, has_side_effects=True, vmem_limit_bytes=66000000),
     )(counts, chosen, gates, tokens, w_gate, w_up, w_down)
+    return jnp.dot(place, answers, preferred_element_type=jnp.float32).astype(bf16)
 
 
 def solution(mesh):

time: 47.3 us -> 43.1 us (0.911)
  Pallas kernels: 44.2 us -> 39.9 us
  matrix products: 0 us -> 3.05 us
  local copies, waits for them, and re-layouts: 2.85 us -> 0 us
    pallas_call x1, Pallas kernels: 44.2 us -> 39.9 us  [shards(): pl.pallas_call(functools.partial(kernel, (n_node, n_local, chunks, tok_de...]
    dot_general x0 -> x1, matrix products: none -> 3.05 us  [shards(): jnp.dot(place, answers, preferred_element_type=jnp.float32).astype(bf16)]
    unnamed x1 -> x0, local copies, waits for them, and re-layouts: 2.85 us -> none
where the time goes in v2:
time: 43.1 us; the launch traced here: 42.9 us
  Pallas kernels  39.9 us (93%)
  matrix products  3.05 us (7%)
    pallas_call x1, Pallas kernels, shards(): pl.pallas_call(functools.partial(kernel, (n_node, n_local, chunks, tok_de...  39.9 us
    dot_general x1, matrix products, shards(): jnp.dot(place, answers, preferred_element_type=jnp.float32).astype(bf16)  3.05 us

profile of v2, /device:TPU:0, one launch (start us, length us, event | category | flops | bytes accessed | tf_op | source)
XLA Modules:
  0.0 42.9 jit_solution(5504162826252578122)
XLA Ops:
  0.0 39.9 %shard_map.73 = (bf16[64,7168]{1,0:T(8,128)(2,1)}, bf16[128,64]{1,0:T(8,128)(2,1)}) custom-call(s32[8]{0:T(128)} %counts_hbm.1, s32[8,48]{1,0:T(8,128)} %chosen_hbm.1, f32[8,48]{1,0:T(8,128)} %gates_hbm.1, bf16[128,7168]{1,0:T(8,128)(2,1)} %tokens_hbm.1, bf16[1,7168,256]{2,1,0:T(8,128)(2,1)} %wg_hbm.1, bf16[1,7168,256]{2,1,0:T(8,128)(2,1)} %wu_hbm.1, ...), custom_call_target="tpu_custom_call" | custom-call | tf_op jit(solution)/shard_map/pallas_call | solution.py:289
  39.9 3.0 %convolution_convert_fusion = bf16[128,7168]{1,0:T(8,128)(2,1)} fusion(bf16[128,64]{1,0:T(8,128)(2,1)} %get-tuple-element.7, bf16[64,7168]{1,0:T(8,128)(2,1)} %get-tuple-element.8), kind=kOutput, calls=%fused_computation | convolution fusion | flops 118358016 | bytes 2768896 | tf_op jit(solution)/shard_map/dot_general | solution.py:323
